TPU v7x, 128 devices: a whole 4x4x4 slice. The times are simulated.
128 devices in a mesh: dp: 1, sp: 128 (over z, y, x, core).
Axes of the slice: x: 4, y: 4, z: 4, core: 2. Of those that a mesh axis runs over, the one named last changes fastest.
Arguments:
- hidden: bfloat16 [2048, 5120], P(('dp', 'sp'))
- seg_ids: int32 [2048], P(('dp', 'sp'))
- positions: int32 [2048], P(('dp', 'sp'))
- prefix_lat: bfloat16 [2048, 576], P(('dp', 'sp'))
- prefix_seg: int32 [2048], P(('dp', 'sp'))
- w_dq: bfloat16 [5120, 1536], replicated
- gain_q: bfloat16 [1536], replicated
- w_uq: bfloat16 [1536, 24576], replicated
- w_dkv: bfloat16 [5120, 576], replicated
- gain_kv: bfloat16 [512], replicated
- w_ukv: bfloat16 [512, 32768], replicated
- w_o: bfloat16 [16384, 5120], replicated
Outputs:
- output: bfloat16 [2048, 5120], P(('dp', 'sp'))
All inputs are finite; a program needn't handle non-finite values.
Results may differ from a plain program's by a relative error of at most 0.00583197.
Values are sent between devices in bfloat16 or wider.
A program may use at most 1.25 GiB of HBM per device.

v0:
```python
import jax
import jax.numpy as jnp
from jax import lax
from jax.sharding import PartitionSpec as P

KV_LAT = 512
ROPE_DIM = 64
NOPE_DIM = 128
V_DIM = 128
QK_DIM = NOPE_DIM + ROPE_DIM
KV_HEAD = NOPE_DIM + V_DIM
ROW_BUDGET = 2048
EPS = 1e-6
ROPE_BASE = 10000.0
NEG_BIG = -1e30


def rms_norm(values, gain):
    inv_rms = lax.rsqrt(jnp.mean(values * values, axis=-1, keepdims=True) + EPS)
    return values * inv_rms * gain.astype(jnp.float32)


def rope_tables(positions):
    half_dim = ROPE_DIM // 2
    inv_freq = ROPE_BASE ** (-jnp.arange(half_dim, dtype=jnp.float32) / half_dim)
    angles = positions.astype(jnp.float32)[:, None] * inv_freq[None, :]
    return jnp.cos(angles), jnp.sin(angles)


def rope_apply(values, cos_t, sin_t):
    half_dim = ROPE_DIM // 2
    lower_half = values[..., :half_dim]
    upper_half = values[..., half_dim:]
    return jnp.concatenate([lower_half * cos_t - upper_half * sin_t, upper_half * cos_t + lower_half * sin_t], axis=-1)


def latent_stage(hidden, positions, w_dq, gain_q, w_dkv, gain_kv):
    q_lat = rms_norm(jnp.dot(hidden, w_dq, preferred_element_type=jnp.float32), gain_q).astype(jnp.bfloat16)
    kv_down = jnp.dot(hidden, w_dkv, preferred_element_type=jnp.float32)
    cos_t, sin_t = rope_tables(positions)
    kv_lat = rms_norm(kv_down[:, :KV_LAT], gain_kv).astype(jnp.bfloat16)
    key_rope = rope_apply(kv_down[:, KV_LAT:], cos_t, sin_t).astype(jnp.bfloat16)
    return q_lat, jnp.concatenate([kv_lat, key_rope], axis=1)


def head_attention(q_lat, q_pos, q_seg, key_lat, key_seg, key_pos, w_uq_part, w_ukv_part, head_count):
    tokens = q_lat.shape[0]
    q_full = jnp.einsum("tc,chd->thd", q_lat, w_uq_part.reshape(-1, head_count, QK_DIM), preferred_element_type=jnp.float32)
    cos_t, sin_t = rope_tables(q_pos)
    q_nope = q_full[..., :NOPE_DIM].astype(jnp.bfloat16)
    q_rope = rope_apply(q_full[..., NOPE_DIM:], cos_t[:, None, :], sin_t[:, None, :]).astype(jnp.bfloat16)
    kv_up = jnp.einsum("kc,chd->khd", key_lat[:, :KV_LAT], w_ukv_part.reshape(KV_LAT, head_count, KV_HEAD), preferred_element_type=jnp.float32).astype(jnp.bfloat16)
    k_nope = kv_up[..., :NOPE_DIM]
    v_heads = kv_up[..., NOPE_DIM:]
    k_rope = key_lat[:, KV_LAT:]
    q_block = min(tokens, max(1, ROW_BUDGET // head_count))
    n_blocks = tokens // q_block

    def attend(block):
        qn_blk, qr_blk, seg_blk, pos_blk = block
        scores = jnp.einsum("qhd,khd->hqk", qn_blk, k_nope, preferred_element_type=jnp.float32)
        scores = scores + jnp.einsum("qhd,kd->hqk", qr_blk, k_rope, preferred_element_type=jnp.float32)
        allowed = (seg_blk[:, None] == key_seg[None, :]) & (key_pos[None, :] <= pos_blk[:, None])
        scores = jnp.where(allowed[None], scores * QK_DIM ** -0.5, NEG_BIG)
        probs = jax.nn.softmax(scores, axis=-1).astype(jnp.bfloat16)
        return jnp.einsum("hqk,khd->qhd", probs, v_heads, preferred_element_type=jnp.float32).astype(jnp.bfloat16)

    block_outs = lax.map(attend, (q_nope.reshape(n_blocks, q_block, head_count, NOPE_DIM), q_rope.reshape(n_blocks, q_block, head_count, ROPE_DIM), q_seg.reshape(n_blocks, q_block), q_pos.reshape(n_blocks, q_block)))
    return block_outs.reshape(tokens, head_count * V_DIM)


def solution(mesh):
    group_size = mesh.shape["sp"]
    tok_spec = P(("dp", "sp"), None)
    vec_spec = P(("dp", "sp"))
    mat_spec = P(None, None)
    gain_spec = P(None)

    def device_step(hidden, seg_ids, positions, prefix_lat, prefix_seg, w_dq, gain_q, w_uq, w_dkv, gain_kv, w_ukv, w_o):
        q_width = w_dq.shape[1]
        head_dev = w_o.shape[0] // V_DIM // group_size
        q_lat, new_lat = latent_stage(hidden, positions, w_dq, gain_q, w_dkv, gain_kv)
        gathered = lax.all_gather(jnp.concatenate([q_lat, new_lat], axis=1), "sp", axis=0, tiled=True)
        prefix_all = lax.all_gather(prefix_lat, "sp", axis=0, tiled=True)
        seg_all = lax.all_gather(seg_ids, "sp", axis=0, tiled=True)
        pos_all = lax.all_gather(positions, "sp", axis=0, tiled=True)
        prefix_seg_all = lax.all_gather(prefix_seg, "sp", axis=0, tiled=True)
        first_head = lax.axis_index("sp") * head_dev
        w_uq_mine = lax.dynamic_slice_in_dim(w_uq, first_head * QK_DIM, head_dev * QK_DIM, axis=1)
        w_ukv_mine = lax.dynamic_slice_in_dim(w_ukv, first_head * KV_HEAD, head_dev * KV_HEAD, axis=1)
        key_lat = jnp.concatenate([prefix_all, gathered[:, q_width:]], axis=0)
        key_seg = jnp.concatenate([prefix_seg_all, seg_all])
        key_pos = jnp.concatenate([jnp.full(prefix_seg_all.shape, -1, jnp.int32), pos_all])
        heads_out = head_attention(gathered[:, :q_width], pos_all, seg_all, key_lat, key_seg, key_pos, w_uq_mine, w_ukv_mine, head_dev)
        tok_out = lax.all_to_all(heads_out, "sp", 0, 1, tiled=True)
        return jnp.dot(tok_out, w_o, preferred_element_type=jnp.float32).astype(jnp.bfloat16)

    return jax.shard_map(
        device_step,
        mesh=mesh,
        in_specs=(tok_spec, vec_spec, vec_spec, tok_spec, vec_spec, mat_spec, gain_spec, mat_spec, mat_spec, gain_spec, mat_spec, mat_spec),
        out_specs=tok_spec,
        check_vma=False,
    )
```

profile of v0, /device:TPU:65, one launch (start us, length us, event | category | flops | bytes accessed | tf_op | source)
XLA Modules:
  0.0 302.3 jit_solution(9961384267071367351)
XLA Ops:
  6.5 0.0 copy-start
  6.5 0.0 all-gather.5.cloned.1.call-start
  6.6 0.7 convert_element_type.49
  7.3 0.2 copy-done
  7.5 0.0 copy-start.2
  7.5 0.0 copy-start.8
  7.5 0.0 copy-start.9
  7.5 0.0 copy-start.11
  7.5 7.9 %multiply_reduce_fusion = (f32[16]{0:T(128)S(1)}, f32[16,1536]{1,0:T(8,128)S(1)}) fusion(bf16[16,5120]{1,0:T(8,128)(2,1)S(1)} %copy-done, bf16[5120,1536]{1,0:T(8,128)(2,1)} %param.17), kind=kOutput, calls=%fused_computation.46 | convolution fusion | flops 251707376 | bytes 15990848 | tf_op jit(solution)/shard_map/dot_general | solution.py:38
  15.4 0.0 copy-done.2
  15.4 1.6 fusion.53
  17.0 0.0 copy-done.8
  17.0 0.1 multiply_reduce_fusion.1
  17.2 0.0 copy-done.9
  17.2 0.1 multiply_convert_fusion.1
  17.3 0.1 fusion.47
  17.4 0.1 multiply_convert_fusion
  17.5 0.7 concatenate.28
  18.2 0.0 all-gather.5.cloned.1.call-update
  18.2 0.0 all-gather.3.cloned.1.call-start
  18.3 0.7 all-gather.3.cloned.1.call-update
  19.0 0.3 dynamic-update-slice.2
  19.2 0.0 copy-done.10
  19.2 0.2 dynamic-update-slice
  19.5 0.0 copy-done.11
  19.5 0.2 dynamic-update-slice.1
  19.7 67.1 %all-reduce.4 = (s32[2048]{0:T(1024)S(1)}, s32[2048]{0:T(1024)S(1)}, s32[2048]{0:T(1024)S(1)}) all-reduce(s32[2048]{0:T(1024)S(1)} %dynamic-update-slice.2, s32[2048]{0:T(1024)S(1)} %dynamic-update-slice, s32[2048]{0:T(1024)S(1)} %dynamic-update-slice.1), channel_id=1, replica_groups=mesh['dp'=1,'sp'=128] {'sp'}, use_global_device_ids=true, to_apply=%add.3 | all-reduce | flops 6144 | bytes 49152
  86.8 2.4 all-gather.5.cloned.1.call-done
  89.2 2.0 slice.58
  91.2 5.4 %fusion.10 = f32[2048,1,192]{0,2,1:T(8,128)S(1)} fusion(bf16[2048,2112]{1,0:T(8,128)(2,1)} %all-gather.5.cloned.1.call-done, bf16[1536,24576]{1,0:T(8,128)(2,1)} %param.19, s32[]{:T(128)S(6)} %select_n.12), kind=kOutput, calls=%fused_computation.16 | convolution fusion | flops 1207959552 | bytes 8650756 | tf_op jit(solution)/shard_map/tc,chd->thd/dot_general | solution.py:48
  96.6 1.1 copy-done.4
  97.7 1.1 fusion.39
  98.9 56.3 %all-gather.3.cloned.1.call-done = bf16[2048,576]{1,0:T(8,128)(2,1)} async-done(((bf16[16,576]{1,0:T(8,128)(2,1)}), bf16[2048,576]{1,0:T(8,128)(2,1)}) %all-gather.3.cloned.1.call-update) | async-done | bytes 2359312 | tf_op jit(solution)/shard_map/all_gather | solution.py:84
  155.2 3.0 fusion.7
  158.1 0.0 copy-done.5
  158.1 0.0 copy-start.6
  158.2 0.0 copy-start.3
  158.2 13.2 %fusion.20 = f32[2048,4096]{1,0:T(8,128)} fusion(bf16[4096,1,256]{2,0,1:T(8,128)(2,1)S(1)} %fusion.7, f32[2048,1,192]{0,2,1:T(8,128)S(1)} %copy-done.5), kind=kOutput, calls=%fused_computation.22 | convolution fusion | flops 2147483648 | bytes 35127296 | tf_op jit(solution)/shard_map/while/body/eval_jaxpr/qhd,khd->hqk/dot_general | solution.py:61
  171.4 0.0 copy-done.6
  171.4 0.0 copy-done.3
  171.4 24.2 %fusion.52 = (f32[2048]{0:T(1024)S(1)}, f32[1,2048,4096]{2,1,0:T(8,128)}) fusion(bf16[2048,32]{0,1:T(8,128)(2,1)S(1)} %get-tuple-element.29, bf16[2048,32]{0,1:T(8,128)(2,1)S(1)} %get-tuple-element.28, bf16[2048,576]{1,0:T(8,128)(2,1)S(1)} %slice.58, bf16[2048,576]{1,0:T(8,128)(2,1)S(1)} %copy-done.3, f32[2048,4096]{1,0:T(8,128)} %fusion.20, ...), kind=kOutput, calls=%fused_computation.67 | convolution fusion | flops 1134032896 | bytes 72146944 | tf_op jit(solution)/shard_map/while/body/eval_jaxpr/qhd,kd->hqk/dot_general | solution.py:62
  195.6 13.7 %fusion.2 = f32[2048]{0:T(1024)S(1)} fusion(f32[1,2048,4096]{2,1,0:T(8,128)} %get-tuple-element.48, f32[2048]{0:T(1024)S(1)} %get-tuple-element.46), kind=kLoop, calls=%fused_computation.5 | loop fusion | flops 16775168 | bytes 33570816 | tf_op jit(solution)/shard_map/while/body/eval_jaxpr/reduce_sum | solution.py:65
  209.3 0.0 copy-done.7
  209.3 14.1 %fusion.16 = bf16[2048,1,128]{0,2,1:T(8,128)(2,1)S(1)} fusion(f32[2048]{0:T(1024)S(1)} %fusion.2, f32[1,2048,4096]{2,1,0:T(8,128)} %get-tuple-element.48, f32[2048]{0:T(1024)S(1)} %get-tuple-element.46, bf16[4096,1,256]{2,0,1:T(8,128)(2,1)S(1)} %copy-done.7), kind=kOutput, calls=%fused_computation.18 | convolution fusion | flops 2172911616 | bytes 35143680 | tf_op jit(solution)/shard_map/while/body/eval_jaxpr/hqk,khd->qhd/dot_general | solution.py:66
  223.4 0.3 copy.15
  223.7 18.4 %all_to_all.19 = bf16[128,16,128]{2,1,0:T(8,128)(2,1)S(1)} all-to-all(bf16[128,16,128]{2,1,0:T(8,128)(2,1)S(1)} %bitcast.57), channel_id=1, replica_groups=mesh['dp'=1,'sp'=128] {'sp'}, dimensions={0} | all-to-all | bytes 1048576 | tf_op jit(solution)/shard_map/all_to_all | solution.py:95
  242.2 53.3 %convolution_convert_fusion = bf16[16,5120]{1,0:T(8,128)(2,1)} fusion(bf16[16384,5120]{1,0:T(8,128)(2,1)} %param.23, bf16[128,16,128]{2,1,0:T(8,128)(2,1)S(1)} %all_to_all.19), kind=kOutput, calls=%fused_computation.10 | convolution fusion | flops 2684436480 | bytes 168460288 | tf_op jit(solution)/shard_map/dot_general | solution.py:96
  295.5 0.0 copy-done.1
  (16 shorter events, 0.1 us)
Async XLA Ops:
  6.5 0.9 copy-start
  6.5 82.7 %all-gather.5.cloned.1.call-start = ((), (), s32[]{:S(2)}) async-start(), calls=%async_computation.2 | async-start | bytes 8982528 | tf_op jit(solution)/shard_map/all_gather | solution.py:83
  7.5 7.9 %copy-start.2 = (bf16[5120,576]{0,1:T(8,128)(2,1)S(1)}, bf16[5120,576]{0,1:T(8,128)(2,1)}, u32[]{:S(2)}) copy-start(bf16[5120,576]{0,1:T(8,128)(2,1)} %param.20) | copy-start | bytes 17694724
  7.5 9.5 %copy-start.8 = (bf16[512]{0:T(512)(128)(2,1)S(1)}, bf16[512]{0:T(512)(128)(2,1)}, u32[]{:S(2)}) copy-start(bf16[512]{0:T(512)(128)(2,1)} %param.21) | copy-start | bytes 3076
  7.5 9.7 %copy-start.9 = (s32[16]{0:T(128)S(1)}, s32[16]{0:T(128)}, u32[]{:S(2)}) copy-start(s32[16]{0:T(128)} %param.14) | copy-start | bytes 196
  7.5 11.8 %copy-start.10 = (s32[16]{0:T(128)S(1)}, s32[16]{0:T(128)}, u32[]{:S(2)}) copy-start(s32[16]{0:T(128)} %param.13) | copy-start | bytes 196
  7.5 12.0 %copy-start.11 = (s32[16]{0:T(128)S(1)}, s32[16]{0:T(128)}, u32[]{:S(2)}) copy-start(s32[16]{0:T(128)} %param.16) | copy-start | bytes 196
  18.2 137.0 %all-gather.3.cloned.1.call-start = ((), (), s32[]{:S(2)}) async-start(), calls=%async_computation.1 | async-start | bytes 2641920 | tf_op jit(solution)/shard_map/all_gather | solution.py:84
  96.6 1.2 copy-start.4
  155.2 3.0 copy-start.5
  158.1 13.2 %copy-start.6 = (bf16[4096,1,256]{2,0,1:T(8,128)(2,1)}, bf16[4096,1,256]{2,0,1:T(8,128)(2,1)S(1)}, u32[]{:S(2)}) copy-start(bf16[4096,1,256]{2,0,1:T(8,128)(2,1)S(1)} %fusion.7) | copy-start | bytes 6291460
  158.2 13.2 %copy-start.3 = (bf16[2048,576]{1,0:T(8,128)(2,1)S(1)}, bf16[2048,576]{1,0:T(8,128)(2,1)}, u32[]{:S(2)}) copy-start(bf16[2048,576]{1,0:T(8,128)(2,1)} %all-gather.3.cloned.1.call-done) | copy-start | bytes 7077892
  195.6 13.7 %copy-start.7 = (bf16[4096,1,256]{2,0,1:T(8,128)(2,1)S(1)}, bf16[4096,1,256]{2,0,1:T(8,128)(2,1)}, u32[]{:S(2)}) copy-start(bf16[4096,1,256]{2,0,1:T(8,128)(2,1)} %copy-done.6) | copy-start | bytes 6291460
  242.2 53.3 %copy-start.1 = (bf16[16,5120]{1,0:T(8,128)(2,1)S(1)}, bf16[16,5120]{1,0:T(8,128)(2,1)}, u32[]{:S(2)}) copy-start(bf16[16,5120]{1,0:T(8,128)(2,1)} %param.12) | copy-start | bytes 491524
Sparse Core Ops, SparseCore 0:
  18.3 70.8 all-gather.4
  92.3 62.7 all-gather.2
where the time goes:
time: 306 us; the launch traced here: 302 us
  matrix products  123 us (40%)
  blocking collectives  85.6 us (28%)
  waiting for transfers between devices  59.4 us (19%)
  other arithmetic  16 us (5%)
  between operations  13.6 us (4%)
  local copies, waits for them, and re-layouts  5.03 us (2%)
    unnamed x1, blocking collectives  67.1 us
    all_gather x1, waiting for transfers between devices, device_step(): prefix_all = lax.all_gather(prefix_lat, 'sp', axis=0, tiled=True)  56.3 us
    dot_general x1, matrix products, device_step(): jnp.dot(tok_out, w_o, preferred_element_type=jnp.float32)  53.3 us
    dot_general x1, matrix products, attend(): jnp.einsum('qhd,kd->hqk', qr_blk, k_rope, preferred_element_type=jnp.floa...  24.2 us
    all_to_all x1, blocking collectives, device_step(): tok_out = lax.all_to_all(heads_out, 'sp', 0, 1, tiled=True)  18.4 us
    dot_general x1, matrix products, attend(): jnp.einsum('hqk,khd->qhd', probs, v_heads, preferred_element_type=jnp.flo...  14.1 us
    reduce_sum x1, other arithmetic, attend(): probs = jax.nn.softmax(scores, axis=-1).astype(jnp.bfloat16)  13.7 us
    dot_general x1, matrix products, attend(): jnp.einsum('qhd,khd->hqk', qn_blk, k_nope, preferred_element_type=jnp.flo...  13.2 us
  transfers between devices with their start and end apart: 2, of which 2 were waited for; matrix products, arithmetic and copies ran while one was open for 3% of the time, Pallas kernels for 0%

commit v1 on v0

v1 whole, which is shorter than its diff:
```python
import functools

import jax
import jax.numpy as jnp
from jax import lax
from jax.experimental import pallas as pl
from jax.experimental.pallas import tpu as pltpu
from jax.sharding import PartitionSpec as P

MESH = pl.DeviceIdType.MESH
KV_LAT = 512
ROPE_DIM = 64
NOPE_DIM = 128
V_DIM = 128
QK_DIM = NOPE_DIM + ROPE_DIM
KV_HEAD = NOPE_DIM + V_DIM
EPS = 1e-6
ROPE_BASE = 10000.0
NEG_BIG = -1e30
LOG2E = 1.4426950408889634
RING = 4
ROWS = 16
PLANE_TOKENS = 512
HEADS_DEV = 4
KV_WIDTH = 640
META = KV_LAT + ROPE_DIM
KEY_BLOCK = 512
W_SLOTS = 8
Q_CHUNKS = 8
KV_CHUNKS = 4


def place():
    me = lax.axis_index("sp")
    core = lax.rem(me, 2)
    x = lax.rem(me // 2, RING)
    y = lax.rem(me // 8, RING)
    z = me // 32
    return z, y, x, core


def index_of(z, y, x, core):
    return ((z * RING + y) * RING + x) * 2 + core


def greet(peers):
    barrier = pltpu.get_barrier_semaphore()
    for peer in peers:
        pl.semaphore_signal(barrier, inc=1, device_id={"sp": peer}, device_id_type=MESH)
    pl.semaphore_wait(barrier, len(peers))


class Stream:
    def __init__(self, slot, ref, axes, order, lanes, sems, first=None):
        self.slot, self.ref, self.axes, self.order, self.lanes, self.first = slot, ref, axes, order, lanes, first
        self.send_sem, self.recv_sem, self.swap_send, self.swap_recv = sems
        z, y, x, self.core = place()
        self.at = (z, y, x)
        self.sent = []

    def view(self, full, core, moved=None):
        index = []
        for axis in self.axes:
            if axis in full:
                index.append(pl.ds(0, RING))
            elif moved is not None and moved[0] == axis:
                index.append(moved[1])
            else:
                index.append(self.at[axis])
        return self.ref.at[tuple(index) + (core, slice(None), self.lanes)]

    def back(self, axis, off):
        return lax.rem(self.at[axis] + RING - off, RING)

    def copy(self, src, dst, send, recv, device):
        return pltpu.make_async_remote_copy(src_ref=src, dst_ref=dst, send_sem=send, recv_sem=recv, device_id={"sp": device}, device_id_type=MESH)

    def send(self, phase):
        axis = self.order[phase]
        for off in (1, 3, 2):
            to = list(self.at)
            to[axis] = lax.rem(self.at[axis] + off, RING)
            mine = self.view(self.order[:phase], self.core)
            src = self.first if phase == 0 and self.first is not None else mine
            c = self.copy(src, mine, self.send_sem.at[self.slot, phase, off - 1], self.recv_sem.at[self.slot, phase, off - 1], index_of(*to, self.core))
            c.start()
            self.sent.append(c)

    def wait(self, phase, off):
        axis = self.order[phase]
        got = self.view(self.order[:phase], self.core, (axis, self.back(axis, off)))
        self.copy(got, got, self.send_sem.at[self.slot, phase, off - 1], self.recv_sem.at[self.slot, phase, off - 1], index_of(*self.at, self.core)).wait_recv()

    def swap(self, off):
        axis = self.order[-1]
        part = self.view(self.order[:-1], self.core, (axis, self.back(axis, off)))
        c = self.copy(part, part, self.swap_send.at[self.slot, off], self.swap_recv.at[self.slot, off], index_of(*self.at, 1 - self.core))
        c.start()
        self.sent.append(c)

    def start(self):
        self.send(0)

    def step(self, phase):
        for off in (1, 3, 2):
            self.wait(phase - 1, off)
        self.send(phase)
        if phase == len(self.order) - 1:
            self.swap(0)

    def finish(self):
        for off in (1, 3, 2):
            self.wait(len(self.order) - 1, off)
            self.swap(off)

    def done(self):
        axis = self.order[-1]
        for off in (0, 1, 3, 2):
            part = self.view(self.order[:-1], 1 - self.core, (axis, self.back(axis, off)))
            self.copy(part, part, self.swap_send.at[self.slot, off], self.swap_recv.at[self.slot, off], index_of(*self.at, 1 - self.core)).wait_recv()
        for c in self.sent:
            c.wait_send()


def rms_norm(values, gain):
    inv_rms = lax.rsqrt(jnp.mean(values * values, axis=-1, keepdims=True) + EPS)
    return values * inv_rms * gain.astype(jnp.float32)


def turn(values, cos_sin):
    half = ROPE_DIM // 2
    swapped = jnp.concatenate([values[:, half:], values[:, :half]], axis=1)
    return values * cos_sin[:, :ROPE_DIM] + swapped * cos_sin[:, ROPE_DIM:]


def gather_kernel(
    hid, pre, meta, cs, gain_q, gain_kv, wdq_hbm, wdkv_hbm,
    kv_out, cq_out, cs_out, cnt_out,
    kv_buf, cq_buf, cs_buf, wq_buf, wkv_buf, wq_sem, wkv_sem, send_sem, recv_sem, swap_send, swap_recv, out_sem,
):
    z, y, x, core = place()
    depth = hid.shape[1]
    q_step, kv_step = depth // Q_CHUNKS, depth // KV_CHUNKS
    kv_loads = [pltpu.make_async_copy(wdkv_hbm.at[pl.ds(k * kv_step, kv_step)], wkv_buf.at[pl.ds(k * kv_step, kv_step)], wkv_sem.at[k]) for k in range(KV_CHUNKS)]
    q_loads = [pltpu.make_async_copy(wdq_hbm.at[pl.ds(k * q_step, q_step)], wq_buf.at[pl.ds(k * q_step, q_step)], wq_sem.at[k]) for k in range(Q_CHUNKS)]
    for c in kv_loads + q_loads:
        c.start()

    peers = [index_of(z, y, x, 1 - core)]
    for off in (1, 2, 3):
        peers.append(index_of(lax.rem(z + off, RING), y, x, core))
        peers.append(index_of(z, lax.rem(y + off, RING), x, core))
        peers.append(index_of(z, y, lax.rem(x + off, RING), core))
    greet(peers)

    sems = (send_sem, recv_sem, swap_send, swap_recv)
    lanes = (pl.ds(0, 256), pl.ds(256, 256), pl.ds(512, 128))
    orders = ((2, 1, 0), (1, 0, 2), (0, 2, 1))
    space = (0, 1, 2)
    plane = (1, 2)
    old = [Stream(i, kv_buf.at[0], space, orders[i], lanes[i], sems, pre.at[:, lanes[i]]) for i in range(3)]
    new = [Stream(3 + i, kv_buf.at[1], space, orders[i], lanes[i], sems) for i in range(3)]
    half = cq_buf.shape[-1] // 2
    lat = [Stream(6, cq_buf, plane, (2, 1), pl.ds(0, half), sems), Stream(7, cq_buf, plane, (1, 2), pl.ds(half, half), sems)]
    turns = [Stream(8, cs_buf, plane, (2, 1), pl.ds(0, 128), sems, cs)]

    for s in old + turns:
        s.start()
    kv_buf[0, z, y, x, core] = pre[...]
    cs_buf[y, x, core] = cs[...]

    down = jnp.zeros((ROWS, META), jnp.float32)
    for k in range(KV_CHUNKS):
        kv_loads[k].wait()
        part = pl.ds(k * kv_step, kv_step)
        down = down + jnp.dot(hid[:, part], wkv_buf[part, :], preferred_element_type=jnp.float32)
    kv_lat = rms_norm(down[:, :KV_LAT], gain_kv[...]).astype(jnp.bfloat16)
    key_rope = turn(down[:, KV_LAT:], cs[...]).astype(jnp.bfloat16)
    kv_buf[1, z, y, x, core] = jnp.concatenate([kv_lat, key_rope, meta[...]], axis=1)
    for s in old + turns:
        s.step(1)
    for s in new:
        s.start()

    q_lat = jnp.zeros((ROWS, wq_buf.shape[1]), jnp.float32)
    for k in range(Q_CHUNKS):
        q_loads[k].wait()
        part = pl.ds(k * q_step, q_step)
        q_lat = q_lat + jnp.dot(hid[:, part], wq_buf[part, :], preferred_element_type=jnp.float32)
        if k == Q_CHUNKS // 2 - 1:
            for s in old:
                s.step(2)
            for s in turns:
                s.finish()
            for s in new:
                s.step(1)
    cq_buf[y, x, core] = rms_norm(q_lat, gain_q[...]).astype(jnp.bfloat16)
    for s in lat:
        s.start()
    for s in new:
        s.step(2)
    for s in old:
        s.finish()
    for s in lat:
        s.step(1)

    def counts(sec):
        tail = kv_buf[sec, :, :, :, :, :, pl.ds(512, 128)].reshape(-1, 128).astype(jnp.float32)
        cnt_out[pl.ds(sec, 1), :] = jnp.sum(tail, axis=0, keepdims=True)

    outs = []
    for s in old + turns:
        s.done()
    outs.append(pltpu.make_async_copy(kv_buf.at[0], kv_out.at[0], out_sem.at[0]))
    outs.append(pltpu.make_async_copy(cs_buf, cs_out, out_sem.at[1]))
    for c in outs:
        c.start()
    counts(0)
    for s in new:
        s.finish()
    for s in new:
        s.done()
    outs.append(pltpu.make_async_copy(kv_buf.at[1], kv_out.at[1], out_sem.at[2]))
    outs[-1].start()
    counts(1)
    for s in lat:
        s.finish()
    for s in lat:
        s.done()
    outs.append(pltpu.make_async_copy(cq_buf, cq_out, out_sem.at[3]))
    outs[-1].start()
    for c in outs:
        c.wait()


def gather_latents(hidden, pre, meta, cs, gain_q, gain_kv, w_dq, w_dkv):
    depth, q_width = w_dq.shape
    kv_shape = (2, RING, RING, RING, 2, ROWS, KV_WIDTH)
    cq_shape = (RING, RING, 2, ROWS, q_width)
    cs_shape = (RING, RING, 2, ROWS, 128)
    vmem = pl.BlockSpec(memory_space=pltpu.VMEM)
    hbm = pl.BlockSpec(memory_space=pl.ANY)
    return pl.pallas_call(
        gather_kernel,
        name="gather_latents",
        out_shape=(
            jax.ShapeDtypeStruct(kv_shape, jnp.bfloat16),
            jax.ShapeDtypeStruct(cq_shape, jnp.bfloat16),
            jax.ShapeDtypeStruct(cs_shape, jnp.float32),
            jax.ShapeDtypeStruct((2, 128), jnp.float32),
        ),
        in_specs=[vmem] * 6 + [hbm] * 2,
        out_specs=(hbm, hbm, hbm, vmem),
        scratch_shapes=[
            pltpu.VMEM(kv_shape, jnp.bfloat16),
            pltpu.VMEM(cq_shape, jnp.bfloat16),
            pltpu.VMEM(cs_shape, jnp.float32),
            pltpu.VMEM((depth, q_width), jnp.bfloat16),
            pltpu.VMEM((depth, META), jnp.bfloat16),
            pltpu.SemaphoreType.DMA((Q_CHUNKS,)),
            pltpu.SemaphoreType.DMA((KV_CHUNKS,)),
            pltpu.SemaphoreType.DMA((9, 3, 3)),
            pltpu.SemaphoreType.DMA((9, 3, 3)),
            pltpu.SemaphoreType.DMA((9, 4)),
            pltpu.SemaphoreType.DMA((9, 4)),
            pltpu.SemaphoreType.DMA((4,)),
        ],
        compiler_params=pltpu.CompilerParams(collective_id=0, has_side_effects=True, vmem_limit_bytes=56 * 1024 * 1024),
    )(hidden, pre, meta, cs, gain_q, gain_kv, w_dq, w_dkv)


def attend_kernel(
    cnt, cs_hbm, cq_hbm, kv_hbm, wuq_hbm, wukv_hbm, out,
    cs, cq, kv, wuq, wukv, wk, wvt, q_all, m_all, l_all, acc, sems,
):
    z, y, x, core = place()
    block = core * (RING * RING) + y * RING + x
    loads = [
        pltpu.make_async_copy(wuq_hbm.at[:, pl.ds(pl.multiple_of(block * HEADS_DEV * QK_DIM, 128), HEADS_DEV * QK_DIM)], wuq, sems.at[0]),
        pltpu.make_async_copy(cq_hbm, cq, sems.at[1]),
        pltpu.make_async_copy(cs_hbm, cs, sems.at[2]),
        pltpu.make_async_copy(wukv_hbm.at[:, pl.ds(pl.multiple_of(block * HEADS_DEV * KV_HEAD, 128), HEADS_DEV * KV_HEAD)], wukv, sems.at[3]),
        pltpu.make_async_copy(kv_hbm, kv, sems.at[4]),
    ]
    for c in loads:
        c.start()
    total = kv.shape[0] // 2
    tokens = cq.shape[0]
    n0 = total - cnt[1, META - 512].astype(jnp.int32)
    p0 = total - cnt[0, META - 512].astype(jnp.int32)
    first = z * tokens
    t = first + lax.broadcasted_iota(jnp.int32, (1, tokens), 1)
    second = t >= n0
    old_lo, old_hi = jnp.where(second, p0, 0), jnp.where(second, total, p0)
    new_lo, new_hi = jnp.where(second, total + n0, total), total + t + 1
    has0, has1 = first < n0, first + tokens > n0
    old_from = jnp.where(has0, 0, p0) // KEY_BLOCK
    old_n = (jnp.where(has1, total, p0) + KEY_BLOCK - 1) // KEY_BLOCK - old_from
    new_from = (total + jnp.where(has0, 0, n0)) // KEY_BLOCK
    new_n = (total + first + tokens) // KEY_BLOCK - new_from

    for c in loads[:3]:
        c.wait()
    q = jnp.dot(cq[...], wuq[...], preferred_element_type=jnp.float32)
    for h in range(HEADS_DEV):
        at = h * QK_DIM
        rope = turn(q[:, at + NOPE_DIM : at + QK_DIM], cs[...]).astype(jnp.bfloat16)
        q_all[h] = jnp.concatenate([q[:, at : at + NOPE_DIM].astype(jnp.bfloat16), rope, jnp.zeros_like(rope)], axis=1)
    loads[3].wait()
    for h in range(HEADS_DEV):
        at = h * KV_HEAD
        wk[:, h * 128 : h * 128 + 128] = wukv[:, at : at + NOPE_DIM]
        wvt[h * 128 : h * 128 + 128, :] = wukv[:, at + NOPE_DIM : at + KV_HEAD].T
    m_all[...] = jnp.full(m_all.shape, NEG_BIG, jnp.float32)
    l_all[...] = jnp.zeros(l_all.shape, jnp.float32)
    acc[...] = jnp.zeros(acc.shape, jnp.float32)
    loads[4].wait()
    scale = QK_DIM ** -0.5 * LOG2E
    nt = (((1,), (1,)), ((), ()))

    def body(i, carry):
        is_old = i < old_n
        row = pl.multiple_of(jnp.where(is_old, old_from + i, new_from + i - old_n) * KEY_BLOCK, KEY_BLOCK)
        lo = jnp.where(is_old, old_lo, new_lo)
        hi = jnp.where(is_old, old_hi, new_hi)
        key = row + lax.broadcasted_iota(jnp.int32, (KEY_BLOCK, tokens), 0)
        allowed = (key >= lo) & (key < hi)
        latent = kv[pl.ds(row, KEY_BLOCK), :KV_LAT]
        tail = kv[pl.ds(row, KEY_BLOCK), KV_LAT:]
        k_all = jnp.dot(latent, wk[...], preferred_element_type=jnp.float32).astype(jnp.bfloat16)
        vt = lax.dot_general(wvt[...], latent, nt, preferred_element_type=jnp.float32).astype(jnp.bfloat16)
        for h in range(HEADS_DEV):
            k = jnp.concatenate([k_all[:, h * 128 : h * 128 + 128], tail], axis=1)
            s = lax.dot_general(k, q_all[h], nt, preferred_element_type=jnp.float32)
            s = jnp.where(allowed, s, NEG_BIG)
            m_old = m_all[h]
            m_new = jnp.maximum(m_old, jnp.max(s, axis=0, keepdims=True))
            p = jnp.exp2((s - m_new) * scale)
            fade = jnp.exp2((m_old - m_new) * scale)
            m_all[h] = m_new
            l_all[h] = l_all[h] * fade + jnp.sum(p, axis=0, keepdims=True)
            acc[h] = acc[h] * fade + jnp.dot(vt[h * 128 : h * 128 + 128, :], p.astype(jnp.bfloat16), preferred_element_type=jnp.float32)
        return carry

    lax.fori_loop(0, old_n + new_n, body, 0)
    for h in range(HEADS_DEV):
        out[:, h * 128 : h * 128 + 128] = (acc[h] / l_all[h]).T.astype(jnp.bfloat16)


def attend(cnt, cs, cq, kv, w_uq, w_ukv):
    tokens, q_width = cq.shape
    hbm = pl.BlockSpec(memory_space=pl.ANY)
    return pl.pallas_call(
        attend_kernel,
        name="attend",
        out_shape=jax.ShapeDtypeStruct((tokens, HEADS_DEV * V_DIM), jnp.bfloat16),
        in_specs=[pl.BlockSpec(memory_space=pltpu.SMEM)] + [hbm] * 5,
        out_specs=pl.BlockSpec(memory_space=pltpu.VMEM),
        scratch_shapes=[
            pltpu.VMEM(cs.shape, jnp.float32),
            pltpu.VMEM(cq.shape, jnp.bfloat16),
            pltpu.VMEM(kv.shape, jnp.bfloat16),
            pltpu.VMEM((q_width, HEADS_DEV * QK_DIM), jnp.bfloat16),
            pltpu.VMEM((KV_LAT, HEADS_DEV * KV_HEAD), jnp.bfloat16),
            pltpu.VMEM((KV_LAT, HEADS_DEV * NOPE_DIM), jnp.bfloat16),
            pltpu.VMEM((HEADS_DEV * V_DIM, KV_LAT), jnp.bfloat16),
            pltpu.VMEM((HEADS_DEV, tokens, 256), jnp.bfloat16),
            pltpu.VMEM((HEADS_DEV, 1, tokens), jnp.float32),
            pltpu.VMEM((HEADS_DEV, 1, tokens), jnp.float32),
            pltpu.VMEM((HEADS_DEV, V_DIM, tokens), jnp.float32),
            pltpu.SemaphoreType.DMA((5,)),
        ],
        compiler_params=pltpu.CompilerParams(vmem_limit_bytes=56 * 1024 * 1024),
    )(cnt, cs, cq, kv, w_uq, w_ukv)


def project_kernel(o_in, wo_hbm, y_out, o_buf, w_buf, acc, other, w_sem, send_sem, recv_sem, swap_sem):
    z, y, x, core = place()
    chip = y * RING + x
    pairs = RING * RING
    depth = w_buf.shape[1]
    base = core * (pairs * depth)

    def sender(s):
        return lax.rem(y + RING - s // RING, RING) * RING + lax.rem(x + RING - lax.rem(s, RING), RING)

    def load(s):
        row = pl.multiple_of(base + sender(s) * depth, depth)
        return pltpu.make_async_copy(wo_hbm.at[pl.ds(row, depth)], w_buf.at[lax.rem(s, W_SLOTS)], w_sem.at[lax.rem(s, W_SLOTS)])

    for s in range(W_SLOTS):
        load(s).start()
    partner = index_of(z, y, x, 1 - core)
    spots = [(lax.rem(y + s // RING, RING), lax.rem(x + s % RING, RING)) for s in range(pairs)]
    greet([partner] + [index_of(z, py, px, core) for py, px in spots[1:]])
    sent = []
    for s in range(1, pairs):
        py, px = spots[s]
        row = pl.multiple_of((py * RING + px) * 2 * ROWS, 2 * ROWS)
        c = pltpu.make_async_remote_copy(
            src_ref=o_in.at[pl.ds(row, 2 * ROWS)], dst_ref=o_buf.at[chip], send_sem=send_sem.at[s], recv_sem=recv_sem.at[s],
            device_id={"sp": index_of(z, py, px, core)}, device_id_type=MESH,
        )
        c.start()
        sent.append(c)
    acc[...] = jnp.zeros(acc.shape, jnp.float32)
    cols = 1024

    def add(s, rows):
        load(s).wait()
        for n in range(acc.shape[1] // cols):
            at = slice(n * cols, n * cols + cols)
            acc[:, at] += jnp.dot(rows, w_buf[lax.rem(s, W_SLOTS), :, at], preferred_element_type=jnp.float32)

    o_buf[chip] = o_in[pl.ds(pl.multiple_of(chip * 2 * ROWS, 2 * ROWS), 2 * ROWS), :]

    def body(s, carry):
        @pl.when(s > 0)
        def _():
            got = o_buf.at[sender(s)]
            pltpu.make_async_remote_copy(src_ref=got, dst_ref=got, send_sem=send_sem.at[s], recv_sem=recv_sem.at[s], device_id={"sp": partner}, device_id_type=MESH).wait_recv()

        add(s, o_buf[sender(s)])

        @pl.when(s + W_SLOTS < pairs)
        def _():
            load(s + W_SLOTS).start()

        return carry

    lax.fori_loop(0, pairs, body, 0)
    theirs = acc.at[pl.ds(pl.multiple_of((1 - core) * ROWS, ROWS), ROWS)]
    c = pltpu.make_async_remote_copy(src_ref=theirs, dst_ref=other, send_sem=swap_sem.at[0], recv_sem=swap_sem.at[1], device_id={"sp": partner}, device_id_type=MESH)
    c.start()
    for k in sent:
        k.wait_send()
    c.wait()
    y_out[...] = (acc[pl.ds(pl.multiple_of(core * ROWS, ROWS), ROWS), :] + other[...]).astype(y_out.dtype)


def project(heads, w_o):
    width = w_o.shape[1]
    depth = heads.shape[1]
    return pl.pallas_call(
        project_kernel,
        name="project",
        out_shape=jax.ShapeDtypeStruct((ROWS, width), jnp.bfloat16),
        in_specs=[pl.BlockSpec(memory_space=pltpu.VMEM), pl.BlockSpec(memory_space=pl.ANY)],
        out_specs=pl.BlockSpec(memory_space=pltpu.VMEM),
        scratch_shapes=[
            pltpu.VMEM((RING * RING, 2 * ROWS, depth), jnp.bfloat16),
            pltpu.VMEM((W_SLOTS, depth, width), jnp.bfloat16),
            pltpu.VMEM((2 * ROWS, width), jnp.float32),
            pltpu.VMEM((ROWS, width), jnp.float32),
            pltpu.SemaphoreType.DMA((W_SLOTS,)),
            pltpu.SemaphoreType.DMA((RING * RING,)),
            pltpu.SemaphoreType.DMA((RING * RING,)),
            pltpu.SemaphoreType.DMA((2,)),
        ],
        compiler_params=pltpu.CompilerParams(collective_id=1, has_side_effects=True, vmem_limit_bytes=60 * 1024 * 1024),
    )(heads, w_o)


def solution(mesh):
    tok_spec = P(("dp", "sp"), None)
    vec_spec = P(("dp", "sp"))
    mat_spec = P(None, None)
    gain_spec = P(None)

    def device_step(hidden, seg_ids, positions, prefix_lat, prefix_seg, w_dq, gain_q, w_uq, w_dkv, gain_kv, w_ukv, w_o):
        half = ROPE_DIM // 2
        inv_freq = ROPE_BASE ** (-jnp.arange(half, dtype=jnp.float32) / half)
        angles = positions.astype(jnp.float32)[:, None] * inv_freq[None, :]
        cos_t, sin_t = jnp.cos(angles), jnp.sin(angles)
        cs = jnp.concatenate([cos_t, cos_t, -sin_t, sin_t], axis=1)
        spare = KV_WIDTH - META
        meta = jnp.pad(seg_ids.astype(jnp.bfloat16)[:, None], ((0, 0), (0, spare - 1)))
        pre = jnp.concatenate([prefix_lat, jnp.pad(prefix_seg.astype(jnp.bfloat16)[:, None], ((0, 0), (0, spare - 1)))], axis=1)
        kv, cq, cs_all, cnt = gather_latents(hidden, pre, meta, cs, gain_q[None, :], gain_kv[None, :], w_dq, w_dkv)
        heads = attend(cnt, cs_all.reshape(-1, 128), cq.reshape(-1, cq.shape[-1]), kv.reshape(-1, KV_WIDTH), w_uq, w_ukv)
        return project(heads, w_o)

    return jax.shard_map(
        device_step,
        mesh=mesh,
        in_specs=(tok_spec, vec_spec, vec_spec, tok_spec, vec_spec, mat_spec, gain_spec, mat_spec, mat_spec, gain_spec, mat_spec, mat_spec),
        out_specs=tok_spec,
        check_vma=False,
    )
```

time: 306 us -> 117 us (0.38)
  matrix products: 123 us -> 0 us
  Pallas kernels: 0 us -> 98.1 us
  blocking collectives: 85.6 us -> 0 us
  waiting for transfers between devices: 59.4 us -> 0 us
  between operations: 13.6 us -> 0.03 us
  other arithmetic: 16 us -> 4.19 us
  local copies, waits for them, and re-layouts: 5.03 us -> 13.6 us
    dot_general x8 -> x0, matrix products: 123 us -> none  [the longest x1 53.3 us: device_step(): jnp.dot(tok_out, w_o, preferred_element_type=jnp.float32)]
    pallas_call x0 -> x3, Pallas kernels: none -> 98.1 us  [the longest x1 39.5 us: gather_latents(): pl.pallas_call(gather_kernel, name='gather_latents', out_shape=(jax.Shape...]
    unnamed x1 -> x0, blocking collectives: 67.1 us -> none
    all_gather x2 -> x0, waiting for transfers between devices: 58.7 us -> none  [the longest x1 56.3 us: device_step(): prefix_all = lax.all_gather(prefix_lat, 'sp', axis=0, tiled=True)]
    all_to_all x1 -> x0, blocking collectives: 18.4 us -> none  [device_step(): tok_out = lax.all_to_all(heads_out, 'sp', 0, 1, tiled=True)]
    reduce_sum x2 -> x0, other arithmetic: 13.8 us -> none  [the longest x1 13.7 us: attend(): probs = jax.nn.softmax(scores, axis=-1).astype(jnp.bfloat16)]
    unnamed x30 -> x2, local copies, waits for them, and re-layouts: 2.08 us -> 10.3 us
  transfers between devices with their start and end apart: 2 -> 0, of which waited for: 2 -> 0; matrix products, arithmetic and copies ran while one was open for 3% -> 0% of each run, Pallas kernels for 0% -> 0%
where the time goes in v1:
time: 117 us; the launch traced here: 116 us
  Pallas kernels  98.1 us (84%)
  local copies, waits for them, and re-layouts  13.6 us (12%)
  other arithmetic  4.19 us (4%)
    pallas_call x1, Pallas kernels, gather_latents(): pl.pallas_call(gather_kernel, name='gather_latents', out_shape=(jax.Shape...  39.5 us
    pallas_call x1, Pallas kernels, project(): pl.pallas_call(project_kernel, name='project', out_shape=jax.ShapeDtypeSt...  30 us
    pallas_call x1, Pallas kernels, attend(): pl.pallas_call(attend_kernel, name='attend', out_shape=jax.ShapeDtypeStru...  28.7 us
    unnamed x2, local copies, waits for them, and re-layouts  10.3 us

profile of v1, /device:TPU:65, one launch (start us, length us, event | category | flops | bytes accessed | tf_op | source)
XLA Modules:
  0.0 116.0 jit_solution(17916843250444655187)
XLA Ops:
  0.0 0.7 convert_bitcast_fusion
  0.7 0.7 convert_element_type.14
  1.3 0.7 convert_bitcast_fusion.1
  2.0 1.3 %broadcast_in_dim.17.gain_kv = bf16[1,512]{1,0:T(2,128)(2,1)} reshape(bf16[512]{0:T(512)(128)(2,1)} %param.21) | data formatting | bytes 2048 | tf_op jit(solution)/shard_map/broadcast_in_dim | solution.py:479
  3.2 0.1 copy.13
  3.3 0.1 copy.14
  3.4 0.6 pad.8.meta
  4.0 1.3 %broadcast_in_dim.16.gain_q = bf16[1,1536]{1,0:T(2,128)(2,1)} reshape(bf16[1536]{0:T(1024)(128)(2,1)} %param.18) | data formatting | bytes 6144 | tf_op jit(solution)/shard_map/broadcast_in_dim | solution.py:479
  5.3 1.4 %fusion.1.pre = bf16[16,640]{1,0:T(8,128)(2,1)} fusion(bf16[16,1]{1,0:T(8,128)(2,1)S(1)} %copy.13, bf16[16,576]{1,0:T(8,128)(2,1)} %param.15), kind=kLoop, calls=%fused_computation.2 | loop fusion | flops 61440 | bytes 38944 | tf_op jit(solution)/shard_map/concatenate | solution.py:478
  6.7 0.1 multiply_cosine_fusion
  6.9 0.7 pad_maximum_fusion.cs
  7.5 8.7 %copy.15.wdkv_hbm = bf16[5120,576]{1,0:T(8,128)(2,1)} copy(bf16[5120,576]{0,1:T(8,128)(2,1)} %param.20) | data formatting | bytes 11796480 | tf_op args[8]
  16.2 39.5 %gather_latents.1 = (bf16[2,4,4,4,2,16,640]{6,5,4,3,2,1,0:T(8,128)(2,1)}, bf16[4,4,2,16,1536]{4,3,2,1,0:T(8,128)(2,1)}, f32[4,4,2,16,128]{4,3,2,1,0:T(8,128)}, f32[2,128]{1,0:T(2,128)}) custom-call(bf16[16,5120]{1,0:T(8,128)(2,1)} %hid.1, bf16[16,640]{1,0:T(8,128)(2,1)} %fusion.1.pre, bf16[16,64]{1,0:T(8,128)(2,1)} %pad.8.meta, ...), custom_call_target="tpu_custom_call" | custom-call | tf_op jit(solution)/shard_map/gather_latents/pallas_call | solution.py:243
  55.7 28.7 %attend.1.o_in = bf16[512,512]{1,0:T(8,128)(2,1)} custom-call(f32[2,128]{1,0:T(2,128)} %get-tuple-element.9.cnt, f32[512,128]{1,0:T(8,128)} %bitcast.9, bf16[512,1536]{1,0:T(8,128)(2,1)} %bitcast.8, bf16[4096,640]{1,0:T(8,128)(2,1)} %bitcast.7, bf16[1536,24576]{1,0:T(8,128)(2,1)} %wuq_hbm.1, bf16[512,32768]{1,0:T(8,128)(2,1)} %wukv_hbm.1), custom_call_target="tpu_custom_call" | custom-call | tf_op jit(solution)/shard_map/attend/pallas_call | solution.py:353
  84.4 30.0 %project.1 = bf16[16,5120]{1,0:T(8,128)(2,1)} custom-call(bf16[512,512]{1,0:T(8,128)(2,1)} %attend.1.o_in, bf16[16384,5120]{1,0:T(8,128)(2,1)} %wo_hbm.1), custom_call_target="tpu_custom_call" | custom-call | tf_op jit(solution)/shard_map/project/pallas_call | solution.py:444
  114.4 1.6 %copy.17 = bf16[16,5120]{1,0:T(8,128)(2,1)} copy(bf16[16,5120]{1,0:T(8,128)(2,1)} %project.1) | data formatting | bytes 327680
  (1 shorter events, 0.0 us)

commit v2 on v1

v2 whole, which is shorter than its diff:
```python
import jax
import jax.numpy as jnp
import numpy as np
from jax import lax
from jax.experimental import pallas as pl
from jax.experimental.pallas import tpu as pltpu
from jax.sharding import PartitionSpec as P

MESH = pl.DeviceIdType.MESH
KV_LAT = 512
ROPE_DIM = 64
NOPE_DIM = 128
V_DIM = 128
QK_DIM = NOPE_DIM + ROPE_DIM
KV_HEAD = NOPE_DIM + V_DIM
EPS = 1e-6
ROPE_BASE = 10000.0
NEG_BIG = -1e30
LOG2E = 1.4426950408889634
RING = 4
ROWS = 16
PLANE_TOKENS = 512
HEADS_DEV = 4
KV_WIDTH = 640
META = KV_LAT + ROPE_DIM
SPARE = KV_WIDTH - META
KEY_BLOCK = 512
W_AHEAD = 6
W_SLOTS = 4
Q_CHUNKS = 8
KV_CHUNKS = ((0, 256), (256, 256), (512, 64))


def near(array):
    return pltpu.with_memory_space_constraint(array, pltpu.VMEM)


def far(array):
    return pltpu.with_memory_space_constraint(array, pltpu.HBM)


def place():
    me = lax.axis_index("sp")
    core = lax.rem(me, 2)
    x = lax.rem(me // 2, RING)
    y = lax.rem(me // 8, RING)
    z = me // 32
    return z, y, x, core


def index_of(z, y, x, core):
    return ((z * RING + y) * RING + x) * 2 + core


def greet(peers):
    barrier = pltpu.get_barrier_semaphore()
    for peer in peers:
        pl.semaphore_signal(barrier, inc=1, device_id={"sp": peer}, device_id_type=MESH)
    pl.semaphore_wait(barrier, len(peers))


class Stream:
    def __init__(self, slot, ref, axes, order, lanes, sems):
        self.slot, self.ref, self.axes, self.order, self.lanes = slot, ref, axes, order, lanes
        self.send_sem, self.recv_sem, self.swap_send, self.swap_recv = sems
        z, y, x, self.core = place()
        self.at = (z, y, x)
        self.sent = []

    def view(self, full, core, moved=None, half=None):
        index = []
        for axis in self.axes:
            if axis in full:
                both = half is None or axis != full[0]
                index.append(pl.ds(0, RING) if both else pl.ds(half * (RING // 2), RING // 2))
            elif moved is not None and moved[0] == axis:
                index.append(moved[1])
            else:
                index.append(self.at[axis])
        return self.ref.at[tuple(index) + (core, slice(None), self.lanes)]

    def back(self, axis, off):
        return lax.rem(self.at[axis] + RING - off, RING)

    def ahead(self, axis, off):
        to = list(self.at)
        to[axis] = lax.rem(self.at[axis] + off, RING)
        return index_of(*to, self.core)

    def copy(self, part, phase, slot, device):
        return pltpu.make_async_remote_copy(
            src_ref=part, dst_ref=part, send_sem=self.send_sem.at[self.slot, phase, slot], recv_sem=self.recv_sem.at[self.slot, phase, slot],
            device_id={"sp": device}, device_id_type=MESH,
        )

    def push(self, part, phase, slot, device):
        c = self.copy(part, phase, slot, device)
        c.start()
        self.sent.append(c)

    def swap_copy(self, off, core):
        part = self.view(self.order[:-1], core, (self.order[-1], self.back(self.order[-1], off)))
        return pltpu.make_async_remote_copy(
            src_ref=part, dst_ref=part, send_sem=self.swap_send.at[self.slot, off], recv_sem=self.swap_recv.at[self.slot, off],
            device_id={"sp": index_of(*self.at, 1 - self.core)}, device_id_type=MESH,
        )

    def swap(self, off):
        c = self.swap_copy(off, self.core)
        c.start()
        self.sent.append(c)

    def send(self, phase):
        last = phase == len(self.order) - 1
        mine = self.view(self.order[:phase], self.core)
        for off in (1, 3) if last else (1, 3, 2):
            self.push(mine, phase, off - 1, self.ahead(self.order[phase], off))
        if last:
            self.swap(0)

    def wait(self, phase, off):
        axis = self.order[phase]
        got = self.view(self.order[:phase], self.core, (axis, self.back(axis, off)))
        self.copy(got, phase, off - 1, self.ahead(axis, 1)).wait_recv()

    def step(self, phase):
        for off in (1, 3, 2):
            self.wait(phase - 1, off)
        self.send(phase)

    def relay(self):
        last = len(self.order) - 1
        axis = self.order[last]
        for off, half, slot in ((1, 0, 1), (3, 1, 3)):
            self.wait(last, off)
            part = self.view(self.order[:last], self.core, (axis, self.back(axis, off)), half)
            self.push(part, last, slot, self.ahead(axis, off))
            self.swap(off)

    def finish(self):
        last = len(self.order) - 1
        axis = self.order[last]
        for half, slot in ((0, 1), (1, 3)):
            part = self.view(self.order[:last], self.core, (axis, self.back(axis, 2)), half)
            self.copy(part, last, slot, self.ahead(axis, 1)).wait_recv()
        self.swap(2)

    def done(self):
        for off in (0, 1, 3, 2):
            self.swap_copy(off, 1 - self.core).wait_recv()
        for c in self.sent:
            c.wait_send()


def rms_norm(values, gain):
    inv_rms = lax.rsqrt(jnp.mean(values * values, axis=-1, keepdims=True) + EPS)
    return values * inv_rms * gain


def turn(values, cos_sin):
    half = ROPE_DIM // 2
    swapped = jnp.concatenate([values[:, half:], values[:, :half]], axis=1)
    return values * cos_sin[:, :ROPE_DIM] + swapped * cos_sin[:, ROPE_DIM:]


def rows_of(scalars, width):
    row = lax.broadcasted_iota(jnp.int32, (ROWS, width), 0)
    values = jnp.zeros((ROWS, width), jnp.int32)
    for r in range(ROWS):
        values = jnp.where(row == r, scalars[r], values)
    return values


def prompt_flags(seg):
    values = rows_of(seg, SPARE)
    lane = lax.broadcasted_iota(jnp.int32, values.shape, 1)
    return ((lane < 2) & (lane == values)).astype(jnp.float32).astype(jnp.bfloat16)


def gather_kernel(
    pos_hbm, seg_hbm, old_seg_hbm, hid_hbm, old_lat_hbm, freq_hbm, gain_q_hbm, gain_kv_hbm, wdq_hbm, wdkv_hbm,
    kv_buf, cq_buf, cs_buf,
    pos, seg, old_seg, hid, old_lat, freq, gain_q, gain_kv, small_sem, wq_buf, wkv_buf, wq_sem, wkv_sem, send_sem, recv_sem, swap_send, swap_recv,
):
    z, y, x, core = place()
    depth = hid_hbm.shape[1]
    q_step = depth // Q_CHUNKS
    kv_loads = [pltpu.make_async_copy(wdkv_hbm.at[pl.ds(at, n)], wkv_buf.at[pl.ds(at, n)], wkv_sem.at[k]) for k, (at, n) in enumerate(KV_CHUNKS)]
    q_loads = [pltpu.make_async_copy(wdq_hbm.at[pl.ds(k * q_step, q_step)], wq_buf.at[pl.ds(k * q_step, q_step)], wq_sem.at[k]) for k in range(Q_CHUNKS)]
    pairs = (
        (pos_hbm, pos), (old_seg_hbm, old_seg), (old_lat_hbm, old_lat), (freq_hbm, freq),
        (seg_hbm, seg), (hid_hbm, hid), (gain_kv_hbm, gain_kv), (gain_q_hbm, gain_q),
    )
    small = [pltpu.make_async_copy(src, dst, small_sem.at[k]) for k, (src, dst) in enumerate(pairs)]
    for c in small + kv_loads + q_loads:
        c.start()
    for c in small:
        c.wait()

    kv_buf[0, z, y, x, core] = jnp.concatenate([old_lat[...], prompt_flags(old_seg)], axis=1)
    angles = rows_of(pos, 128).astype(jnp.float32) * freq[...]
    lane = lax.broadcasted_iota(jnp.int32, angles.shape, 1)
    sines = jnp.sin(angles)
    cs = jnp.where(lane < ROPE_DIM, jnp.cos(angles), jnp.where(lane < ROPE_DIM + ROPE_DIM // 2, -sines, sines))
    cs_buf[y, x, core] = cs

    peers = [index_of(z, y, x, 1 - core)]
    for off in (1, 2, 3):
        peers.append(index_of(lax.rem(z + off, RING), y, x, core))
        peers.append(index_of(z, lax.rem(y + off, RING), x, core))
        peers.append(index_of(z, y, lax.rem(x + off, RING), core))
    greet(peers)

    sems = (send_sem, recv_sem, swap_send, swap_recv)
    lanes = (pl.ds(0, 256), pl.ds(256, 256), pl.ds(512, 128))
    space = (0, 1, 2)
    plane = (1, 2)
    to_z, to_y, to_x = (2, 1, 0), (0, 2, 1), (1, 0, 2)
    old = [Stream(i, kv_buf.at[0], space, (to_z, to_x, to_y)[i], lanes[i], sems) for i in range(3)]
    new = [Stream(3 + i, kv_buf.at[1], space, (to_z, to_y, to_x)[i], lanes[i], sems) for i in range(3)]
    half = cq_buf.shape[-1] // 2
    lat = [Stream(6, cq_buf, plane, (2, 1), pl.ds(0, half), sems), Stream(7, cq_buf, plane, (1, 2), pl.ds(half, half), sems)]
    turns = [Stream(8, cs_buf, plane, (2, 1), pl.ds(0, 128), sems)]
    for s in old + turns:
        s.send(0)

    nt = (((1,), (1,)), ((), ()))
    down = []
    for k, (at, n) in enumerate(KV_CHUNKS):
        kv_loads[k].wait()
        down.append(lax.dot_general(hid[...], wkv_buf[at : at + n, :], nt, preferred_element_type=jnp.float32))
    kv_lat = rms_norm(jnp.concatenate(down[:-1], axis=1), gain_kv[...].astype(jnp.float32).reshape(1, -1)).astype(jnp.bfloat16)
    key_rope = turn(down[-1], cs).astype(jnp.bfloat16)
    kv_buf[1, z, y, x, core] = jnp.concatenate([kv_lat, key_rope, prompt_flags(seg)], axis=1)
    for s in old + turns:
        s.step(1)
    for s in new:
        s.send(0)

    q_lat = jnp.zeros((ROWS, wq_buf.shape[1]), jnp.float32)
    for k in range(Q_CHUNKS):
        q_loads[k].wait()
        part = pl.ds(k * q_step, q_step)
        q_lat = q_lat + jnp.dot(hid[:, part], wq_buf[part, :], preferred_element_type=jnp.float32)
        if k == 4:
            for s in old:
                s.step(2)
            for s in new:
                s.step(1)
    cq_buf[y, x, core] = rms_norm(q_lat, gain_q[...].astype(jnp.float32).reshape(1, -1)).astype(jnp.bfloat16)
    for s in lat:
        s.send(0)
    for s in turns + old:
        s.relay()
    for s in new:
        s.step(2)
    for s in lat:
        s.step(1)
    for s in turns + old:
        s.finish()
    for s in new + lat:
        s.relay()
    for s in new + lat:
        s.finish()
    for s in turns + old + new + lat:
        s.done()


def gather_latents(positions, seg_ids, prefix_seg, hidden, prefix_lat, gain_q, gain_kv, w_dq, w_dkv_t):
    depth, q_width = w_dq.shape
    half = ROPE_DIM // 2
    freq = np.float32(ROPE_BASE) ** (-np.arange(half, dtype=np.float32) / np.float32(half))
    freq = np.tile(freq, 128 // half)[None, :].astype(np.float32)
    vmem = pl.BlockSpec(memory_space=pltpu.VMEM)
    hbm = pl.BlockSpec(memory_space=pl.ANY)
    return pl.pallas_call(
        gather_kernel,
        name="gather_latents",
        out_shape=(
            pltpu.VMEM((2, RING, RING, RING, 2, ROWS, KV_WIDTH), jnp.bfloat16),
            pltpu.VMEM((RING, RING, 2, ROWS, q_width), jnp.bfloat16),
            pltpu.VMEM((RING, RING, 2, ROWS, 128), jnp.float32),
        ),
        in_specs=[hbm] * 10,
        out_specs=(vmem,) * 3,
        scratch_shapes=[
            pltpu.SMEM((ROWS,), jnp.int32),
            pltpu.SMEM((ROWS,), jnp.int32),
            pltpu.SMEM((ROWS,), jnp.int32),
            pltpu.VMEM(hidden.shape, jnp.bfloat16),
            pltpu.VMEM(prefix_lat.shape, jnp.bfloat16),
            pltpu.VMEM(freq.shape, jnp.float32),
            pltpu.VMEM(gain_q.shape, jnp.bfloat16),
            pltpu.VMEM(gain_kv.shape, jnp.bfloat16),
            pltpu.SemaphoreType.DMA((8,)),
            pltpu.VMEM((depth, q_width), jnp.bfloat16),
            pltpu.VMEM((META, depth), jnp.bfloat16),
            pltpu.SemaphoreType.DMA((Q_CHUNKS,)),
            pltpu.SemaphoreType.DMA((len(KV_CHUNKS),)),
            pltpu.SemaphoreType.DMA((9, 3, 4)),
            pltpu.SemaphoreType.DMA((9, 3, 4)),
            pltpu.SemaphoreType.DMA((9, 4)),
            pltpu.SemaphoreType.DMA((9, 4)),
        ],
        compiler_params=pltpu.CompilerParams(collective_id=0, has_side_effects=True, vmem_limit_bytes=24 * 1024 * 1024),
    )(*map(far, (positions, seg_ids, prefix_seg, hidden, prefix_lat, jnp.asarray(freq), gain_q, gain_kv, w_dq, w_dkv_t)))


def sender(z, y, x, s):
    return lax.rem(y + RING - s // RING, RING) * RING + lax.rem(x + RING - lax.rem(s, RING), RING)


def attend_kernel(
    cs, cq, kv, wuq_hbm, wukv_hbm, wo_hbm, out, w_ahead,
    wuq, wukv, wk, wvt, q_all, m_all, l_all, acc, sems, w_sem,
):
    z, y, x, core = place()
    block = core * (RING * RING) + y * RING + x
    loads = [
        pltpu.make_async_copy(wuq_hbm.at[:, pl.ds(pl.multiple_of(block * HEADS_DEV * QK_DIM, 128), HEADS_DEV * QK_DIM)], wuq, sems.at[0]),
        pltpu.make_async_copy(wukv_hbm.at[:, pl.ds(pl.multiple_of(block * HEADS_DEV * KV_HEAD, 128), HEADS_DEV * KV_HEAD)], wukv, sems.at[1]),
    ]
    depth = w_ahead.shape[1]
    for s in range(W_AHEAD):
        row = pl.multiple_of((core * (RING * RING) + sender(z, y, x, s)) * depth, depth)
        loads.append(pltpu.make_async_copy(wo_hbm.at[pl.ds(row, depth)], w_ahead.at[s], w_sem.at[s]))
    for c in loads:
        c.start()
    total = kv.shape[0] // 2
    tokens = cq.shape[0]

    def first_rows(sec):
        flags = kv[pl.ds(sec * total, total), pl.ds(KV_LAT, 128)].astype(jnp.float32)
        lane = lax.broadcasted_iota(jnp.int32, (1, 128), 1)
        return jnp.sum(jnp.where(lane == ROPE_DIM, jnp.sum(flags, axis=0, keepdims=True), 0.0)).astype(jnp.int32)

    p0, n0 = first_rows(0), first_rows(1)
    first = z * tokens
    has0, has1 = first < n0, first + tokens > n0
    old_from = jnp.where(has0, 0, p0) // KEY_BLOCK
    old_n = (jnp.where(has1, total, p0) + KEY_BLOCK - 1) // KEY_BLOCK - old_from
    new_from = (total + jnp.where(has0, 0, n0)) // KEY_BLOCK
    new_n = (total + first) // KEY_BLOCK - new_from

    token = first + lax.broadcasted_iota(jnp.int32, (tokens, SPARE), 0)
    lane = lax.broadcasted_iota(jnp.int32, (tokens, SPARE), 1)
    other = jnp.where(token >= n0, 0, 1)
    gate = jnp.where(lane == other, NEG_BIG, 0.0).astype(jnp.bfloat16)

    loads[0].wait()
    q = jnp.dot(cq[...], wuq[...], preferred_element_type=jnp.float32)
    for h in range(HEADS_DEV):
        at = h * QK_DIM
        rope = turn(q[:, at + NOPE_DIM : at + QK_DIM], cs[...]).astype(jnp.bfloat16)
        q_all[h] = jnp.concatenate([q[:, at : at + NOPE_DIM].astype(jnp.bfloat16), rope, gate], axis=1)
    loads[1].wait()
    for h in range(HEADS_DEV):
        at = h * KV_HEAD
        wk[:, h * 128 : h * 128 + 128] = wukv[:, at : at + NOPE_DIM]
        wvt[h * 128 : h * 128 + 128, :] = wukv[:, at + NOPE_DIM : at + KV_HEAD].T
    scale = QK_DIM ** -0.5 * LOG2E
    nt = (((1,), (1,)), ((), ()))

    def block_of(row, size, start):
        latent = kv[pl.ds(row, size), :KV_LAT]
        tail = kv[pl.ds(row, size), KV_LAT:]
        k_all = jnp.dot(latent, wk[...], preferred_element_type=jnp.float32).astype(jnp.bfloat16)
        vt = lax.dot_general(wvt[...], latent, nt, preferred_element_type=jnp.float32).astype(jnp.bfloat16)

        def score(h):
            k = jnp.concatenate([k_all[:, h * 128 : h * 128 + 128], tail], axis=1)
            return lax.dot_general(k, q_all[h], nt, preferred_element_type=jnp.float32)

        ahead = score(0)
        for h in range(HEADS_DEV):
            s = ahead
            if h + 1 < HEADS_DEV:
                ahead = score(h + 1)
            v = vt[h * 128 : h * 128 + 128, :]
            if start:
                causal = lax.broadcasted_iota(jnp.int32, s.shape, 0) <= lax.broadcasted_iota(jnp.int32, s.shape, 1)
                s = jnp.where(causal, s, NEG_BIG)
                m_new = jnp.max(s, axis=0, keepdims=True)
                p = jnp.exp2((s - m_new) * scale)
                l_all[h] = jnp.sum(p, axis=0, keepdims=True)
                acc[h] = jnp.dot(v, p.astype(jnp.bfloat16), preferred_element_type=jnp.float32)
            else:
                m_old = m_all[h]
                m_new = jnp.maximum(m_old, jnp.max(s, axis=0, keepdims=True))
                p = jnp.exp2((s - m_new) * scale)
                fade = jnp.exp2((m_old - m_new) * scale)
                l_all[h] = l_all[h] * fade + jnp.sum(p, axis=0, keepdims=True)
                acc[h] = acc[h] * fade + jnp.dot(v, p.astype(jnp.bfloat16), preferred_element_type=jnp.float32)
            m_all[h] = m_new

    block_of(pl.multiple_of(total + first, tokens), tokens, True)

    def body(i, carry):
        row = jnp.where(i < old_n, old_from + i, new_from + i - old_n) * KEY_BLOCK
        block_of(pl.multiple_of(row, KEY_BLOCK), KEY_BLOCK, False)
        return carry

    lax.fori_loop(0, old_n + new_n, body, 0)
    for h in range(HEADS_DEV):
        out[:, h * 128 : h * 128 + 128] = (acc[h] / l_all[h]).T.astype(jnp.bfloat16)
    for c in loads[2:]:
        c.wait()


def attend(cs, cq, kv, w_uq, w_ukv, w_o):
    tokens, q_width = cq.shape
    hbm = pl.BlockSpec(memory_space=pl.ANY)
    vmem = pl.BlockSpec(memory_space=pltpu.VMEM)
    return pl.pallas_call(
        attend_kernel,
        name="attend",
        out_shape=(
            pltpu.VMEM((tokens, HEADS_DEV * V_DIM), jnp.bfloat16),
            pltpu.VMEM((W_AHEAD, HEADS_DEV * V_DIM, w_o.shape[1]), jnp.bfloat16),
        ),
        in_specs=[vmem] * 3 + [hbm] * 3,
        out_specs=(vmem, vmem),
        scratch_shapes=[
            pltpu.VMEM((q_width, HEADS_DEV * QK_DIM), jnp.bfloat16),
            pltpu.VMEM((KV_LAT, HEADS_DEV * KV_HEAD), jnp.bfloat16),
            pltpu.VMEM((KV_LAT, HEADS_DEV * NOPE_DIM), jnp.bfloat16),
            pltpu.VMEM((HEADS_DEV * V_DIM, KV_LAT), jnp.bfloat16),
            pltpu.VMEM((HEADS_DEV, tokens, 256), jnp.bfloat16),
            pltpu.VMEM((HEADS_DEV, 1, tokens), jnp.float32),
            pltpu.VMEM((HEADS_DEV, 1, tokens), jnp.float32),
            pltpu.VMEM((HEADS_DEV, V_DIM, tokens), jnp.float32),
            pltpu.SemaphoreType.DMA((2,)),
            pltpu.SemaphoreType.DMA((W_AHEAD,)),
        ],
        compiler_params=pltpu.CompilerParams(vmem_limit_bytes=14 * 1024 * 1024),
    )(cs, cq, kv, w_uq, w_ukv, w_o)


def project_kernel(o_in, w_ahead, wo_hbm, y_out, o_buf, w_buf, acc, other, w_sem, send_sem, recv_sem, swap_sem):
    z, y, x, core = place()
    chip = y * RING + x
    pairs = RING * RING
    depth = w_buf.shape[1]
    base = core * (pairs * depth)

    def load(s):
        row = pl.multiple_of(base + sender(z, y, x, s) * depth, depth)
        return pltpu.make_async_copy(wo_hbm.at[pl.ds(row, depth)], w_buf.at[lax.rem(s - W_AHEAD, W_SLOTS)], w_sem.at[lax.rem(s - W_AHEAD, W_SLOTS)])

    for s in range(W_SLOTS):
        load(W_AHEAD + s).start()
    partner = index_of(z, y, x, 1 - core)
    spots = [(lax.rem(y + s // RING, RING), lax.rem(x + s % RING, RING)) for s in range(pairs)]
    greet([partner] + [index_of(z, py, px, core) for py, px in spots[1:]])
    sent = []
    for s in range(1, pairs):
        py, px = spots[s]
        row = pl.multiple_of((py * RING + px) * 2 * ROWS, 2 * ROWS)
        c = pltpu.make_async_remote_copy(
            src_ref=o_in.at[pl.ds(row, 2 * ROWS)], dst_ref=o_buf.at[chip], send_sem=send_sem.at[s], recv_sem=recv_sem.at[s],
            device_id={"sp": index_of(z, py, px, core)}, device_id_type=MESH,
        )
        c.start()
        sent.append(c)
    acc[...] = jnp.zeros(acc.shape, jnp.float32)
    cols = 1024

    def add(s, w):
        rows = o_buf[sender(z, y, x, s)]
        for n in range(acc.shape[1] // cols):
            at = slice(n * cols, n * cols + cols)
            acc[:, at] += jnp.dot(rows, w[:, at], preferred_element_type=jnp.float32)

    def arrive(s):
        got = o_buf.at[sender(z, y, x, s)]
        pltpu.make_async_remote_copy(src_ref=got, dst_ref=got, send_sem=send_sem.at[s], recv_sem=recv_sem.at[s], device_id={"sp": partner}, device_id_type=MESH).wait_recv()

    o_buf[chip] = o_in[pl.ds(pl.multiple_of(chip * 2 * ROWS, 2 * ROWS), 2 * ROWS), :]

    def held(s, carry):
        @pl.when(s > 0)
        def _():
            arrive(s)

        add(s, w_ahead.at[s])
        return carry

    def streamed(s, carry):
        arrive(s)
        load(s).wait()
        add(s, w_buf.at[lax.rem(s - W_AHEAD, W_SLOTS)])

        @pl.when(s + W_SLOTS < pairs)
        def _():
            load(s + W_SLOTS).start()

        return carry

    lax.fori_loop(0, W_AHEAD, held, 0)
    lax.fori_loop(W_AHEAD, pairs, streamed, 0)
    theirs = acc.at[pl.ds(pl.multiple_of((1 - core) * ROWS, ROWS), ROWS)]
    c = pltpu.make_async_remote_copy(src_ref=theirs, dst_ref=other, send_sem=swap_sem.at[0], recv_sem=swap_sem.at[1], device_id={"sp": partner}, device_id_type=MESH)
    c.start()
    for k in sent:
        k.wait_send()
    c.wait()
    y_out[...] = (acc[pl.ds(pl.multiple_of(core * ROWS, ROWS), ROWS), :] + other[...]).astype(y_out.dtype)


def project(heads, w_ahead, w_o):
    width = w_o.shape[1]
    depth = heads.shape[1]
    return pl.pallas_call(
        project_kernel,
        name="project",
        out_shape=jax.ShapeDtypeStruct((ROWS, width), jnp.bfloat16),
        in_specs=[pl.BlockSpec(memory_space=pltpu.VMEM)] * 2 + [pl.BlockSpec(memory_space=pl.ANY)],
        out_specs=pl.BlockSpec(memory_space=pltpu.VMEM),
        scratch_shapes=[
            pltpu.VMEM((RING * RING, 2 * ROWS, depth), jnp.bfloat16),
            pltpu.VMEM((W_SLOTS, depth, width), jnp.bfloat16),
            pltpu.VMEM((2 * ROWS, width), jnp.float32),
            pltpu.VMEM((ROWS, width), jnp.float32),
            pltpu.SemaphoreType.DMA((W_SLOTS,)),
            pltpu.SemaphoreType.DMA((RING * RING,)),
            pltpu.SemaphoreType.DMA((RING * RING,)),
            pltpu.SemaphoreType.DMA((2,)),
        ],
        compiler_params=pltpu.CompilerParams(collective_id=1, has_side_effects=True, vmem_limit_bytes=24 * 1024 * 1024),
    )(heads, w_ahead, w_o)


def solution(mesh):
    tok_spec = P(("dp", "sp"), None)
    vec_spec = P(("dp", "sp"))
    mat_spec = P(None, None)
    gain_spec = P(None)

    def device_step(hidden, seg_ids, positions, prefix_lat, prefix_seg, w_dq, gain_q, w_uq, w_dkv, gain_kv, w_ukv, w_o):
        kv, cq, cs = gather_latents(positions, seg_ids, prefix_seg, hidden, prefix_lat, gain_q, gain_kv, w_dq, w_dkv.T)
        heads, w_ahead = attend(near(cs.reshape(-1, 128)), near(cq.reshape(-1, cq.shape[-1])), near(kv.reshape(-1, KV_WIDTH)), w_uq, w_ukv, w_o)
        return project(near(heads), near(w_ahead), w_o)

    return jax.shard_map(
        device_step,
        mesh=mesh,
        in_specs=(tok_spec, vec_spec, vec_spec, tok_spec, vec_spec, mat_spec, gain_spec, mat_spec, mat_spec, gain_spec, mat_spec, mat_spec),
        out_specs=tok_spec,
        check_vma=False,
    )
```

time: 117 us -> 98.3 us (0.84)
  the two profiles are of different devices: /device:TPU:65 before, /device:TPU:97 now
where the time goes in v2:
time: 98.3 us; the launch traced here: 98.2 us
  Pallas kernels  96.5 us (98%)
  local copies, waits for them, and re-layouts  1.59 us (2%)
    pallas_call x1, Pallas kernels, gather_latents(): pl.pallas_call(gather_kernel, name='gather_latents', out_shape=(pltpu.VME...  39 us
    pallas_call x1, Pallas kernels, attend(): pl.pallas_call(attend_kernel, name='attend', out_shape=(pltpu.VMEM((token...  30.1 us
    pallas_call x1, Pallas kernels, project(): pl.pallas_call(project_kernel, name='project', out_shape=jax.ShapeDtypeSt...  27.5 us

profile of v2, /device:TPU:97, one launch (start us, length us, event | category | flops | bytes accessed | tf_op | source)
XLA Modules:
  0.0 98.2 jit_solution(4916269503482054988)
XLA Ops:
  0.0 39.0 %gather_latents.1 = (bf16[2,4,4,4,2,16,640]{6,5,4,3,2,1,0:T(8,128)(2,1)S(1)}, bf16[4,4,2,16,1536]{4,3,2,1,0:T(8,128)(2,1)S(1)}, f32[4,4,2,16,128]{4,3,2,1,0:T(8,128)S(1)}) custom-call(s32[16]{0:T(128)} %pos_hbm.1, s32[16]{0:T(128)} %seg_hbm.1, s32[16]{0:T(128)} %old_seg_hbm.1, bf16[16,5120]{1,0:T(8,128)(2,1)} %hid_hbm.1, bf16[16,576]{1,0:T(8,128)(2,1)} %old_lat_hbm.1, ...), custom_call_target="tpu_custom_call" | custom-call | tf_op jit(solution)/shard_map/gather_latents/pallas_call | solution.py:276
  39.0 30.1 %attend.1 = (bf16[512,512]{1,0:T(8,128)(2,1)S(1)}, bf16[6,512,5120]{2,1,0:T(8,128)(2,1)S(1)}) custom-call(f32[512,128]{1,0:T(8,128)S(1)} %bitcast.6, bf16[512,1536]{1,0:T(8,128)(2,1)S(1)} %bitcast.5, bf16[4096,640]{1,0:T(8,128)(2,1)S(1)} %bitcast.4, bf16[1536,24576]{1,0:T(8,128)(2,1)} %wuq_hbm.1, bf16[512,32768]{1,0:T(8,128)(2,1)} %wukv_hbm.1, ...), custom_call_target="tpu_custom_call" | custom-call | tf_op jit(solution)/shard_map/attend/pallas_call | solution.py:414
  69.1 27.5 %project.1 = bf16[16,5120]{1,0:T(8,128)(2,1)} custom-call(bf16[512,512]{1,0:T(8,128)(2,1)S(1)} %get-tuple-element.13.o_in, bf16[6,512,5120]{2,1,0:T(8,128)(2,1)S(1)} %get-tuple-element.14.w_ahead, bf16[16384,5120]{1,0:T(8,128)(2,1)} %wo_hbm.3), custom_call_target="tpu_custom_call" | custom-call | tf_op jit(solution)/shard_map/project/pallas_call | solution.py:513
  96.6 1.6 %copy.15 = bf16[16,5120]{1,0:T(8,128)(2,1)} copy(bf16[16,5120]{1,0:T(8,128)(2,1)} %project.1) | data formatting | bytes 327680
